TPU v7x, 128 devices: a whole 4x4x4 slice. The times are simulated.
128 devices in a mesh: dom: 128 (over z, x, y, core).
Axes of the slice: x: 4, y: 4, z: 4, core: 2. Of those that a mesh axis runs over, the one named last changes fastest.
Arguments:
- features: bfloat16 [2097152, 256], P('dom'), may hold values from -48 to 48, as said below
- w_first: bfloat16 [1280, 256], replicated, may hold values from -0.15625 to 0.15625
- w_second: bfloat16 [1280, 256], replicated, may hold values from -0.15625 to 0.15625
- seed_owner: int32 [36864, 1], P('dom'), may hold values from 0 to 127; in each aligned block of 288 rows (0 to 287, 288 to 575, ...) at most 5 rows name the same one
- seed_row: int32 [36864], P('dom'), may hold values from 0 to 16383
- hop1_owner: int32 [147456, 1], P('dom'), may hold values from 0 to 127; in each aligned block of 1152 rows (0 to 1151, 1152 to 2303, ...) at most 18 rows name the same one
- hop1_row: int32 [147456], P('dom'), may hold values from 0 to 16383
- hop1_rel: int32 [147456], P('dom'), may hold values from 0 to 3
- hop2_owner: int32 [294912, 1], P('dom'), may hold values from 0 to 127; in each aligned block of 2304 rows (0 to 2303, 2304 to 4607, ...) at most 36 rows name the same one
- hop2_row: int32 [294912], P('dom'), may hold values from 0 to 16383
- hop2_rel: int32 [294912], P('dom'), may hold values from 0 to 3
- edge_mask: int32 [16384], P('dom'), may hold values 0 or 1
Outputs:
- edge_loss: float32 [16384], P('dom')
- mean_loss: float32 [], replicated
Inputs may be any that keep to these rules, and one draw needn't show every extreme that they name: `features`: standard normal entries; in some draws each row is scaled by a factor up to 10. `seed_owner`: among the rows of one device no owner is named by more than 5 rows; some owner is named by exactly 5 in every draw. `hop1_owner`: among the rows of one device no owner is named by more than 18 rows; some owner is named by exactly 18 in every draw. `hop2_owner`: among the rows of one device no owner is named by more than 36 rows; some owner is named by exactly 36 in every draw.
All inputs are finite; a program needn't handle non-finite values. No bound on the sum of `edge_mask` on one device may be relied on, other than what follows from the above.
Results may differ from a plain program's by a relative error of at most 0.002.
Values may be sent and summed in bfloat16 or wider, within the bound.
A program may use at most 64 MiB of HBM per device.

v0:
```python
import functools

import jax
import jax.numpy as jnp
from jax import lax
from jax.sharding import Mesh
from jax.sharding import PartitionSpec as P

R = 4
BLOCK = 128
NEG = 32
FAN1 = 4
FAN2 = 2
DOM = ("dom_0", "dom_1", "dom_2", "dom_3")


def by_axis(value, axes):
    return functools.reduce(lax.psum, axes, value)


def bucket_rows(owner, rows, devices, capacity):
    owners = owner[:, 0]
    length = owners.shape[0]
    onehot = (owners[:, None] == jnp.arange(devices, dtype=jnp.int32)[None, :]).astype(jnp.bfloat16)
    counter = jnp.arange(length, dtype=jnp.int32)
    earlier = (counter[:, None] > counter[None, :]).astype(jnp.bfloat16)
    prior = jnp.dot(earlier, onehot, preferred_element_type=jnp.float32)
    position = jnp.sum(prior * onehot.astype(jnp.float32), axis=1).astype(jnp.int32)
    slot_index = owners * capacity + position
    slot_hot = (
        slot_index[:, None] == jnp.arange(devices * capacity, dtype=jnp.int32)[None, :]
    ).astype(jnp.bfloat16)
    halves = jnp.stack([rows // 128, rows % 128], axis=1).astype(jnp.bfloat16)
    placed = lax.dot_general(
        slot_hot, halves, (((0,), (0,)), ((), ())), preferred_element_type=jnp.float32
    )
    requests = (placed[:, 0] * 128.0 + placed[:, 1]).astype(jnp.int32)
    return (slot_index, requests.reshape(devices, capacity))


def unpack_rows(returned, slot_index):
    return returned[slot_index]


def rgcn_layer(self_rows, neighbours, relations, weights):
    width = self_rows.shape[1]
    onehot = (relations[..., None] == jnp.arange(R, dtype=jnp.int32)).astype(jnp.float32)
    tallies = jnp.maximum(jnp.sum(onehot, axis=1), 1.0)
    shares = onehot / tallies[:, None, :]
    merged = shares[:, 0, :, None] * neighbours[:, 0, None, :].astype(jnp.float32)
    for column in range(1, neighbours.shape[1]):
        merged = merged + shares[:, column, :, None] * neighbours[:, column, None, :].astype(
            jnp.float32
        )
    merged = merged.astype(jnp.bfloat16).reshape(self_rows.shape[0], R * width)
    inputs = jnp.concatenate([self_rows, merged], axis=1)
    return jnp.dot(inputs, weights, preferred_element_type=jnp.float32)


def shards(
    features,
    w_first,
    w_second,
    seed_owner,
    seed_row,
    hop1_owner,
    hop1_row,
    hop1_rel,
    hop2_owner,
    hop2_row,
    hop2_rel,
    edge_mask,
):
    devices = lax.axis_size(DOM)
    width = features.shape[1]
    seed_count = seed_row.shape[0]
    first_count = hop1_row.shape[0]
    positives = edge_mask.shape[0]
    blocks = positives // BLOCK
    cap_seed = (2 * seed_count + devices - 1) // devices
    cap_first = (2 * first_count + devices - 1) // devices
    cap_second = (2 * hop2_row.shape[0] + devices - 1) // devices
    seed_slots, seed_requests = bucket_rows(seed_owner, seed_row, devices, cap_seed)
    first_slots, first_requests = bucket_rows(hop1_owner, hop1_row, devices, cap_first)
    second_slots, second_requests = bucket_rows(hop2_owner, hop2_row, devices, cap_second)
    requests = jnp.concatenate([seed_requests, first_requests, second_requests], axis=1)
    arrived = lax.all_to_all(requests, DOM, split_axis=0, concat_axis=0, tiled=True)
    total_cap = cap_seed + cap_first + cap_second
    located = features[arrived.reshape(-1)].reshape(devices, total_cap, width)
    returned = lax.all_to_all(located, DOM, split_axis=0, concat_axis=0, tiled=True)
    x_seed = unpack_rows(returned[:, :cap_seed].reshape(devices * cap_seed, width), seed_slots)
    x_hop1 = unpack_rows(
        returned[:, cap_seed : cap_seed + cap_first].reshape(devices * cap_first, width),
        first_slots,
    )
    x_hop2 = unpack_rows(
        returned[:, cap_seed + cap_first :].reshape(devices * cap_second, width), second_slots
    )
    first_hop = jax.nn.relu(
        rgcn_layer(
            x_hop1,
            x_hop2.reshape(first_count, FAN2, width),
            hop2_rel.reshape(first_count, FAN2),
            w_first,
        )
    ).astype(jnp.bfloat16)
    first_seed = jax.nn.relu(
        rgcn_layer(
            x_seed,
            x_hop1.reshape(seed_count, FAN1, width),
            hop1_rel.reshape(seed_count, FAN1),
            w_first,
        )
    ).astype(jnp.bfloat16)
    second = rgcn_layer(
        first_seed,
        first_hop.reshape(seed_count, FAN1, width),
        hop1_rel.reshape(seed_count, FAN1),
        w_second,
    )
    sources = second[:positives]
    targets = second[positives : 2 * positives]
    negatives = second[2 * positives :].reshape(blocks, NEG, width)
    positive = jnp.sum(sources * targets, axis=1)
    negative = jnp.einsum("bef,bqf->beq", sources.reshape(blocks, BLOCK, width), negatives).reshape(
        positives, NEG
    )
    scores = jnp.concatenate([positive[:, None], negative], axis=1)
    top_score = jnp.max(scores, axis=1, keepdims=True)
    edge_loss = top_score[:, 0] + jnp.log(jnp.sum(jnp.exp(scores - top_score), axis=1)) - positive
    weights = edge_mask.astype(jnp.float32)
    loss_total, edge_total = (
        by_axis(jnp.sum(weights * edge_loss), DOM),
        by_axis(jnp.sum(weights), DOM),
    )
    mean_loss = loss_total / jnp.maximum(edge_total, 1.0)
    return (edge_loss, mean_loss)


def solution(mesh):
    torus = Mesh(mesh.devices.reshape(4, 4, 4, 2), ("dom_0", "dom_1", "dom_2", "dom_3"))
    return jax.shard_map(
        shards,
        mesh=torus,
        in_specs=(
            P(DOM, None),
            P(),
            P(),
            P(DOM, None),
            P(DOM),
            P(DOM, None),
            P(DOM),
            P(DOM),
            P(DOM, None),
            P(DOM),
            P(DOM),
            P(DOM),
        ),
        out_specs=(P(DOM), P()),
        check_vma=False,
    )
```

profile of v0, /device:TPU:1, one launch (start us, length us, event | category | flops | bytes accessed | tf_op | source)
XLA Modules:
  0.0 208.2 jit_solution(16385916544430833277)
XLA Ops:
  0.6 0.8 reduce.8
  1.5 2.5 %fusion.18 = f32[2304]{0:T(1024)S(1)} fusion(s32[2304]{0:T(1024)S(1)} %reduce.8), kind=kOutput, calls=%fused_computation.23 | convolution fusion | flops 1366030080 | bytes 18432 | tf_op jit(solution)/shard_map/dot_general | solution.py:27
  4.2 7.4 %fusion = f32[4608,2]{0,1:T(2,128)S(1)} fusion(s32[2304]{0:T(1024)S(1)} %get-tuple-element.3, bf16[2304,1]{0,1:T(2,128)(2,1)S(1)} %stack.43, bf16[2304,1]{0,1:T(2,128)(2,1)S(1)} %stack.42), kind=kOutput, calls=%fused_computation.5 | convolution fusion | flops 53102592 | bytes 55296 | tf_op jit(solution)/shard_map/dot_general | solution.py:34
  11.8 0.8 fusion.19
  12.7 2.2 %fusion.3 = f32[2304,2]{0,1:T(2,128)S(1)} fusion(s32[1152]{0:T(1024)S(1)} %get-tuple-element.5, bf16[1152,1]{0,1:T(2,128)(2,1)S(1)} %stack.40, bf16[1152,1]{0,1:T(2,128)(2,1)S(1)} %stack.39), kind=kOutput, calls=%fused_computation.10 | convolution fusion | flops 13280256 | bytes 27648 | tf_op jit(solution)/shard_map/dot_general | solution.py:34
  15.1 0.4 fusion.22
  16.2 20.9 %all_to_all.14 = s32[128,1,59]{2,1,0:T(1,128)S(1)} all-to-all(s32[128,1,59]{2,1,0:T(1,128)S(1)} %bitcast.59), channel_id=1, replica_groups=mesh['dom_0'=4,'dom_1'=4,'dom_2'=4,'dom_3'=2] {'dom_0','dom_1','dom_2','..., dimensions={0} | all-to-all | bytes 60416 | tf_op jit(solution)/shard_map/all_to_all | solution.py:87
  37.2 0.5 broadcast.152
  37.7 0.8 reduce.28
  38.8 22.7 %gather_fusion = bf16[7552,256]{1,0:T(8,128)(2,1)} fusion(bf16[16384,256]{1,0:T(8,128)(2,1)} %param.12, s32[8192]{0:T(1024)S(1)} %pad_clamp_fusion), kind=kCustom, calls=%fused_computation | custom fusion | bytes 7763456 | tf_op jit(solution)/shard_map/gather | solution.py:89
  61.5 6.2 %reshape.180 = bf16[128,59,256]{2,1,0:T(8,128)(2,1)} reshape(bf16[7552,256]{1,0:T(8,128)(2,1)} %gather_fusion) | data formatting | bytes 7733248 | tf_op jit(solution)/shard_map/reshape | solution.py:89
  67.6 5.4 %all-to-all-start.1 = ((bf16[128,59,256]{2,1,0:T(8,128)(2,1)}), bf16[128,59,256]{2,1,0:T(8,128)(2,1)}, u32[]{:S(2)}, u32[]{:S(2)}) async-start(bf16[128,59,256]{2,1,0:T(8,128)(2,1)} %reshape.180), calls=%async_computation.1 | async-start | bytes 8388608 | tf_op jit(solution)/shard_map/all_to_all | solution.py:90
  73.1 0.5 eq.161
  74.0 1.1 copy.22
  75.1 1.1 copy.23
  76.7 0.8 copy.18
  77.5 0.8 copy.19
  78.3 0.8 copy.20
  79.1 0.6 pad_clamp_fusion.3
  79.7 0.6 pad_clamp_fusion.2
  80.3 45.6 %all-to-all-done.1 = bf16[128,59,256]{2,1,0:T(8,128)(2,1)} async-done(((bf16[128,59,256]{2,1,0:T(8,128)(2,1)}), bf16[128,59,256]{2,1,0:T(8,128)(2,1)}, u32[]{:S(2)}, u32[]{:S(2)}) %all-to-all-start.1) | async-done | bytes 3866656 | tf_op jit(solution)/shard_map/all_to_all | solution.py:90
  126.0 5.0 %slice.141 = bf16[128,36,256]{2,1,0:T(8,128)(2,1)} slice(bf16[128,59,256]{2,1,0:T(8,128)(2,1)} %all-to-all-done.1), slice={[0:128], [23:59], [0:256]} | slice | bytes 4718592 | tf_op jit(solution)/shard_map/slice | solution.py:97
  131.0 3.4 %reshape.184 = bf16[4608,256]{1,0:T(8,128)(2,1)S(1)} reshape(bf16[128,36,256]{2,1,0:T(8,128)(2,1)} %slice.141) | data formatting | bytes 4718592 | tf_op jit(solution)/shard_map/reshape | solution.py:97
  134.4 7.4 %gather_fusion.3 = bf16[2304,256]{1,0:T(8,128)(2,1)} fusion(bf16[4608,256]{1,0:T(8,128)(2,1)S(1)} %reshape.184, s32[3072]{0:T(1024)S(1)} %pad_clamp_fusion.1), kind=kCustom, calls=%fused_computation.3 | custom fusion | bytes 2368512 | tf_op jit(solution)/shard_map/gather | solution.py:42
  141.8 2.9 %reshape.185 = bf16[1152,2,256]{2,1,0:T(2,128)(2,1)S(1)} reshape(bf16[2304,256]{1,0:T(8,128)(2,1)} %gather_fusion.3) | data formatting | bytes 2359296 | tf_op jit(solution)/shard_map/reshape | solution.py:102
  144.7 1.7 slice_convert_fusion.1
  146.6 0.9 copy-done.1
  147.6 3.3 %add_convert_fusion = bf16[1152,4,256]{2,1,0:T(4,128)(2,1)S(1)} fusion(f32[1152,256]{1,0:T(8,128)S(1)} %get-tuple-element.49, f32[1152,4]{1,0:T(8,128)S(1)} %copy-done.2, f32[1152,256]{1,0:T(8,128)S(1)} %get-tuple-element.50, f32[1152,4]{1,0:T(8,128)S(1)} %copy-done.1), kind=kLoop, calls=%fused_computation.14 | loop fusion | flops 4718592 | bytes 4755456 | tf_op jit(solution)/shard_map/convert_element_type | solution.py:55
  150.9 2.0 copy.35
  152.9 2.5 %slice.132 = bf16[128,18,256]{2,1,0:T(8,128)(2,1)S(1)} slice(bf16[128,59,256]{2,1,0:T(8,128)(2,1)} %all-to-all-done.1), slice={[0:128], [5:23], [0:256]} | slice | bytes 2359296 | tf_op jit(solution)/shard_map/slice | solution.py:93
  155.4 0.4 reshape.182
  155.8 4.3 %gather_fusion.2 = bf16[1152,256]{1,0:T(8,128)(2,1)S(1)} fusion(bf16[2304,256]{1,0:T(8,128)(2,1)S(1)} %reshape.182, s32[2048]{0:T(1024)} %pad_clamp_fusion.2), kind=kCustom, calls=%fused_computation.2 | custom fusion | bytes 1184256 | tf_op jit(solution)/shard_map/gather | solution.py:42
  160.3 2.6 %fusion.14 = bf16[1152,256]{1,0:T(8,128)(2,1)S(1)} fusion(bf16[1280,256]{1,0:T(8,128)(2,1)S(1)} %copy-done, bf16[1152,1024]{1,0:T(8,128)(2,1)} %bitcast.50, bf16[1152,256]{1,0:T(8,128)(2,1)S(1)} %gather_fusion.2), kind=kOutput, calls=%fused_computation.21 | convolution fusion | flops 761462784 | bytes 4194304 | tf_op jit(solution)/shard_map/dot_general | solution.py:57
  163.1 0.8 slice_convert_fusion.5
  164.0 0.8 slice_convert_fusion.9
  164.9 0.8 copy-done.3
  165.9 2.1 %add_convert_fusion.2 = (bf16[288,4,256]{2,1,0:T(4,128)(2,1)S(1)}, bf16[288,4,256]{2,1,0:T(4,128)(2,1)S(1)}) fusion(f32[288,256]{1,0:T(8,128)S(1)} %get-tuple-element.45, f32[288,4]{1,0:T(8,128)S(1)} %copy-done.5, f32[288,256]{1,0:T(8,128)S(1)} %get-tuple-element.46, f32[288,4]{1,0:T(8,128)S(1)} %copy-done.4, f32[288,256]{1,0:T(8,128)S(1)} %get-tuple-element.47, ...), kind=kLoop, calls=%fused_computation.30 | loop fusion | flops 4718592 | bytes 3557376 | tf_op jit(solution)/shard_map/convert.11
  168.1 1.1 slice.130
  169.4 0.4 copy-done.10
  169.8 2.0 gather_fusion.1
  171.9 0.4 fusion.21
  172.2 0.7 copy-done.16
  172.9 0.4 fusion.26
  173.6 1.1 convert_reduce_fusion.2
  174.7 7.0 %all-reduce.2 = (f32[]{:T(128)}, f32[]{:T(128)}) all-reduce(f32[]{:T(128)} %get-tuple-element.9, f32[]{:T(128)} %get-tuple-element.8), channel_id=1, replica_groups=mesh['dom_0'=4,'dom_1'=4,'dom_2'=4,'dom_3'=2] {'dom_0'}, use_global_device_ids=true, to_apply=%region_9.10 | all-reduce | flops 2 | bytes 16 | tf_op jit(solution)/shard_map/psum | solution.py:18
  181.7 7.9 %all-reduce.1 = (f32[]{:T(128)}, f32[]{:T(128)}) all-reduce(f32[]{:T(128)} %get-tuple-element.14, f32[]{:T(128)} %get-tuple-element.15), channel_id=1, replica_groups=mesh['dom_0'=4,'dom_1'=4,'dom_2'=4,'dom_3'=2] {'dom_1'}, use_global_device_ids=true, to_apply=%region_10.11 | all-reduce | flops 2 | bytes 16 | tf_op jit(solution)/shard_map/psum | solution.py:18
  189.6 6.8 %all-reduce = (f32[]{:T(128)}, f32[]{:T(128)}) all-reduce(f32[]{:T(128)} %get-tuple-element.12, f32[]{:T(128)} %get-tuple-element.13), channel_id=1, replica_groups=mesh['dom_0'=4,'dom_1'=4,'dom_2'=4,'dom_3'=2] {'dom_2'}, use_global_device_ids=true, to_apply=%region_11.12 | all-reduce | flops 2 | bytes 16 | tf_op jit(solution)/shard_map/psum | solution.py:18
  196.4 9.5 %all-reduce.3 = (f32[]{:T(128)}, f32[]{:T(128)}) all-reduce(f32[]{:T(128)} %get-tuple-element.10, f32[]{:T(128)} %get-tuple-element.11), channel_id=1, replica_groups=mesh['dom_0'=4,'dom_1'=4,'dom_2'=4,'dom_3'=2] {'dom_3'}, use_global_device_ids=true, to_apply=%region_12.13 | all-reduce | flops 2 | bytes 16 | tf_op jit(solution)/shard_map/psum | solution.py:18
  (87 shorter events, 3.9 us)
Async XLA Ops:
  0.6 159.7 %copy-start = (bf16[1280,256]{1,0:T(8,128)(2,1)S(1)}, bf16[1280,256]{1,0:T(8,128)(2,1)}, u32[]{:S(2)}) copy-start(bf16[1280,256]{1,0:T(8,128)(2,1)} %param.13) | copy-start | bytes 1966084
  1.4 2.6 %copy-start.6 = (s32[2304,1]{0,1:T(1,128)S(1)}, s32[2304,1]{0,1:T(1,128)}, u32[]{:S(2)}) copy-start(s32[2304,1]{0,1:T(1,128)} %param.20) | copy-start | bytes 27652
  1.5 2.6 %copy-start.8 = (s32[2304]{0:T(1024)S(1)}, s32[2304]{0:T(1024)}, u32[]{:S(2)}) copy-start(s32[2304]{0:T(1024)} %param.21) | copy-start | bytes 27652
  4.2 7.6 %copy-start.7 = (s32[1152,1]{0,1:T(1,128)S(1)}, s32[1152,1]{0,1:T(1,128)}, u32[]{:S(2)}) copy-start(s32[1152,1]{0,1:T(1,128)} %param.17) | copy-start | bytes 13828
  11.8 0.8 copy-start.12
  12.7 2.4 %copy-start.13 = (s32[288,1]{0,1:T(1,128)S(1)}, s32[288,1]{0,1:T(1,128)}, u32[]{:S(2)}) copy-start(s32[288,1]{0,1:T(1,128)} %param.15) | copy-start | bytes 3460
  12.7 2.8 %copy-start.14 = (s32[288]{0:T(512)S(1)}, s32[288]{0:T(512)}, u32[]{:S(2)}) copy-start(s32[288]{0:T(512)} %param.16) | copy-start | bytes 3460
  67.6 5.5 %copy-start.9 = (s32[2304]{0:T(1024)S(1)}, s32[2304]{0:T(1024)}, u32[]{:S(2)}) copy-start(s32[2304]{0:T(1024)} %param.22) | copy-start | bytes 27652
  67.6 58.3 %all-to-all-start.1 = ((bf16[128,59,256]{2,1,0:T(8,128)(2,1)}), bf16[128,59,256]{2,1,0:T(8,128)(2,1)}, u32[]{:S(2)}, u32[]{:S(2)}) async-start(bf16[128,59,256]{2,1,0:T(8,128)(2,1)} %reshape.180), calls=%async_computation.1 | async-start | bytes 8388608 | tf_op jit(solution)/shard_map/all_to_all | solution.py:90
  73.1 3.1 %copy-start.11 = (s32[1152]{0:T(1024)S(1)}, s32[1152]{0:T(1024)}, u32[]{:S(2)}) copy-start(s32[1152]{0:T(1024)} %param.19) | copy-start | bytes 13828
  146.4 1.1 copy-start.1
  146.4 1.2 copy-start.2
  164.8 0.9 copy-start.3
  164.8 1.0 copy-start.4
  164.8 1.0 copy-start.5
  169.2 0.7 copy-start.10
  171.8 1.1 copy-start.16
  172.9 0.7 copy-start.15
where the time goes:
time: 209 us; the launch traced here: 208 us
  local copies, waits for them, and re-layouts  70.9 us (34%)
  blocking collectives  52.1 us (25%)
  waiting for transfers between devices  45.6 us (22%)
  matrix products  17 us (8%)
  other arithmetic  13.5 us (6%)
  starting transfers between devices  5.45 us (3%)
  between operations  3.66 us (2%)
    all_to_all x1, waiting for transfers between devices, shards(): lax.all_to_all(located, DOM, split_axis=0, concat_axis=0, tiled=True)  45.6 us
    psum x4, blocking collectives, by_axis(): return functools.reduce(lax.psum, axes, value)  31.1 us
    gather x1, local copies, waits for them, and re-layouts, shards(): located = features[arrived.reshape(-1)].reshape(devices, total_cap, width)  22.7 us
    all_to_all x1, blocking collectives, shards(): lax.all_to_all(requests, DOM, split_axis=0, concat_axis=0, tiled=True)  20.9 us
    gather x3, local copies, waits for them, and re-layouts, unpack_rows(): return returned[slot_index]  13.8 us
    dot_general x3, matrix products, bucket_rows(): lax.dot_general(slot_hot, halves, (((0,), (0,)), ((), ())), preferred_ele...  9.86 us
    reshape x2, local copies, waits for them, and re-layouts, shards(): located = features[arrived.reshape(-1)].reshape(devices, total_cap, width)  6.38 us
    unnamed x44, local copies, waits for them, and re-layouts  5.68 us
  transfers between devices with their start and end apart: 1, of which 1 were waited for; matrix products, arithmetic and copies ran while one was open for 3% of the time, Pallas kernels for 0%

commit v1 on v0

v1 whole, which is shorter than its diff:
```python
import functools

import jax
import jax.numpy as jnp
from jax import lax
from jax.experimental import pallas as pl
from jax.experimental.pallas import tpu as pltpu
from jax.sharding import PartitionSpec as P

R = 4
FAN1 = 4
FAN2 = 2
LANES = 128
STEP = 45
LOGICAL = pl.DeviceIdType.LOGICAL
F32 = jnp.float32
BF16 = jnp.bfloat16
NT = (((1,), (1,)), ((), ()))


def kernel(
    n, count, caps,
    feat_hbm, wf_hbm, ws_hbm,
    own0_hbm, row0_hbm, own1_hbm, row1_hbm, rel1_hbm, own2_hbm, row2_hbm, rel2_hbm, mask_hbm,
    loss_ref, mean_ref,
    own0, row0, own1, row1, rel1, own2, row2, rel2, mask_ref,
    fbf, fsp, wf, ws, pad_own, pad_row, slots0, slots1, slots2, req_out, req_in,
    send0, send1, send2, recv0, recv1, recv2, x0, x1, x2, min1, min0, h1l, h1r, relc1, relc2,
    part_out, part_in,
    req_s, slot0_s, slot1_s, slot2_s,
    isem, fsem, wsem, qsend, qrecv, ssem, rsem, tsem, psend, precv,
):
    n_seed, n_one, n_two = count
    cap0, cap1, cap2 = caps
    bases = (0, cap0, cap0 + cap1)
    me = lax.axis_index("dom")
    width = wf.shape[1]
    nodes = fbf.shape[0]
    gap = fsp.shape[0] - nodes

    def target(k):
        return lax.rem(me + lax.rem(k * STEP, n), n)

    here_refs = (own2, row2, own1, row1, own0, row0, rel2, rel1, mask_ref)
    there_refs = (
        own2_hbm, row2_hbm, own1_hbm, row1_hbm, own0_hbm, row0_hbm, rel2_hbm, rel1_hbm, mask_hbm
    )
    index_copies = [
        pltpu.make_async_copy(a, b if len(a.shape) == 2 else b.at[0], isem.at[i])
        for i, (a, b) in enumerate(zip(there_refs, here_refs))
    ]
    for copy in index_copies:
        copy.start()

    barrier = pltpu.get_barrier_semaphore()

    def greet(k, _):
        pl.semaphore_signal(barrier, 1, device_id=target(k), device_id_type=LOGICAL)
        return 0

    lax.fori_loop(1, n, greet, 0)
    chunks = fsem.shape[0]
    part = nodes // chunks
    feat_copies = [
        pltpu.make_async_copy(
            feat_hbm.at[pl.ds(i * part, part)], fbf.at[pl.ds(i * part, part)], fsem.at[i]
        )
        for i in range(chunks)
    ]
    for copy in feat_copies:
        copy.start()
    w_copies = [
        pltpu.make_async_copy(wf_hbm, wf, wsem.at[0]),
        pltpu.make_async_copy(ws_hbm, ws, wsem.at[1]),
    ]
    for copy in w_copies:
        copy.start()

    iota_own = lax.broadcasted_iota(jnp.int32, (n, LANES), 0)
    iota_slot = lax.broadcasted_iota(jnp.int32, (64, LANES), 0)
    upper = lax.broadcasted_iota(jnp.int32, (LANES, LANES), 0) < lax.broadcasted_iota(
        jnp.int32, (LANES, LANES), 1
    )
    ladder = jnp.concatenate(
        [jnp.where(upper, 1.0, 0.0).astype(BF16), jnp.ones((LANES, LANES), BF16)], axis=1
    )

    def bucket(owner_ref, row_ref, slots, cap, base, blocks, table):
        def block(b, carry):
            before, table = carry
            cols = pl.ds(pl.multiple_of(b * LANES, LANES), LANES)
            owner = owner_ref[:, cols]
            rows = row_ref[:, cols]
            hot = jnp.where(iota_own == owner, 1.0, 0.0)
            hot16 = hot.astype(BF16)
            counts = jnp.dot(hot16, ladder, preferred_element_type=F32)
            prior = counts[:, :LANES] + before
            place = jnp.sum(hot * prior, axis=0, keepdims=True).astype(jnp.int32)
            place = jnp.clip(place, 0, cap - 1)
            slots[:, cols] = owner * cap + place
            here = iota_slot == place + base
            high = (rows >> 7).astype(F32)
            low = (rows & 127).astype(F32)
            values = jnp.concatenate(
                [jnp.where(here, high, 0.0), jnp.where(here, low, 0.0)], axis=0
            ).astype(BF16)
            table = table + lax.dot_general(hot16, values, NT, preferred_element_type=F32)
            return before + counts[:, LANES:], table

        zero = jnp.zeros((n, LANES), F32)
        return lax.fori_loop(0, blocks, block, (zero, table))[1]

    for copy in index_copies[:6]:
        copy.wait()
    pad_own[...] = jnp.full(pad_own.shape, -1, jnp.int32)
    pad_row[...] = jnp.zeros(pad_row.shape, jnp.int32)
    pad_own[:, :n_seed] = own0[...]
    pad_row[:, :n_seed] = row0[...]
    table = jnp.zeros((n, LANES), F32)
    table = bucket(own2, row2, slots2, cap2, bases[2], n_two // LANES, table)
    table = bucket(own1, row1, slots1, cap1, bases[1], n_one // LANES, table)
    table = bucket(pad_own, pad_row, slots0, cap0, bases[0], pad_own.shape[1] // LANES, table)
    wanted = (table * 128.0 + pltpu.roll(table, 64, 1)).astype(jnp.int32)
    wanted = jnp.clip(wanted, 0, nodes - 1)
    for i in range(n):
        req_out[i] = wanted[i : i + 1]

    def widen(i, _):
        step = 128
        r = pl.multiple_of(i * step, step)
        rows = fbf[pl.ds(r, step), :].astype(F32)
        fsp[pl.ds(r, step), :] = rows[:, :LANES]
        fsp[pl.ds(pl.multiple_of(r + gap, 8), step), :] = rows[:, LANES:]
        return 0

    per_chunk = part // 128
    feat_copies[0].wait()
    lax.fori_loop(0, per_chunk, widen, 0)

    pl.semaphore_wait(barrier, n - 1)

    def ask(k, _):
        t = target(k)
        pltpu.make_async_remote_copy(
            src_ref=req_out.at[t], dst_ref=req_in.at[me], send_sem=qsend, recv_sem=qrecv,
            device_id=t, device_id_type=LOGICAL,
        ).start()
        return 0

    lax.fori_loop(1, n, ask, 0)
    req_in[me] = req_out[me]

    for i in range(1, chunks):
        feat_copies[i].wait()
        lax.fori_loop(i * per_chunk, (i + 1) * per_chunk, widen, 0)

    rest = pl.ds(0, n - 1)
    pltpu.make_async_copy(req_in.at[rest], req_in.at[rest], qrecv).wait()
    small = [
        pltpu.make_async_copy(req_in, req_s, tsem.at[0]),
        pltpu.make_async_copy(slots2, slot2_s, tsem.at[1]),
        pltpu.make_async_copy(slots1, slot1_s, tsem.at[2]),
        pltpu.make_async_copy(slots0, slot0_s, tsem.at[3]),
    ]
    for copy in small:
        copy.start()
    small[0].wait()

    hops = ((send2, recv2, cap2, bases[2], 2), (send1, recv1, cap1, bases[1], 1), (send0, recv0, cap0, bases[0], 0))

    def gather(t, out, cap, base):
        for j in range(cap):
            node = req_s[t, 0, base + j]
            pair = fsp[pl.ds(node, 2, stride=gap), :]
            out[t * cap + j] = pair.astype(BF16)

    def start_send(t, out, into, cap, h):
        pltpu.make_async_remote_copy(
            src_ref=out.at[pl.ds(t * cap, cap)], dst_ref=into.at[pl.ds(me * cap, cap)],
            send_sem=ssem.at[h], recv_sem=rsem.at[h], device_id=t, device_id_type=LOGICAL,
        ).start()

    for out, into, cap, base, h in hops:

        def serve(k, _, out=out, into=into, cap=cap, base=base, h=h):
            gather(target(k), out, cap, base)
            start_send(target(k - 1), out, into, cap, h)
            return 0

        gather(target(1), out, cap, base)
        lax.fori_loop(2, n, serve, 0)
        gather(me, into, cap, base)
        start_send(target(n - 1), out, into, cap, h)

    for copy in index_copies[6:]:
        copy.wait()

    def relation_columns(rel_ref, out, blocks):
        def block(b, _):
            at = pl.multiple_of(b * LANES, LANES)
            row = rel_ref[:, pl.ds(at, LANES)].astype(F32)
            out[pl.ds(at, LANES), :] = jnp.broadcast_to(row, (LANES, LANES)).T
            return 0

        lax.fori_loop(0, blocks, block, 0)

    relation_columns(rel2, relc2, n_two // LANES)
    relation_columns(rel1, relc1, n_one // LANES)
    for copy in small[1:]:
        copy.wait()
    for copy in w_copies:
        copy.wait()

    def unpack(slot_s, came, out, total):
        batch = 32

        def some(b, _):
            for j in range(batch):
                i = b * batch + j
                pair = came[slot_s[0, i]].astype(F32)
                out[pl.ds(pl.multiple_of(i * 2, 2), 2), :] = pair
            return 0

        lax.fori_loop(0, total // batch, some, 0)

    def arrived(h, came, cap):
        got = came.at[pl.ds(0, (n - 1) * cap)]
        pltpu.make_async_copy(got, got, rsem.at[h]).wait()

    arrived(2, recv2, cap2)
    unpack(slot2_s, recv2, x2, n_two)
    tile = 32

    def two_means(b, _):
        f = pl.multiple_of(b * tile, tile)
        ra = relc2[pl.ds(FAN2 * f, tile, stride=FAN2), :]
        rb = relc2[pl.ds(FAN2 * f + 1, tile, stride=FAN2), :]
        share = jnp.where(ra == rb, 0.5, 1.0)
        for half in range(2):
            a = x2[pl.ds(4 * f + half, tile, stride=4), :] * share
            v = x2[pl.ds(4 * f + 2 + half, tile, stride=4), :] * share
            for r in range(R):
                mean = jnp.where(ra == r, a, 0.0) + jnp.where(rb == r, v, 0.0)
                at = r * width + half * LANES
                min1[pl.ds(f, tile), at : at + LANES] = mean.astype(BF16)
        return 0

    lax.fori_loop(0, n_one // tile, two_means, 0)

    arrived(1, recv1, cap1)
    unpack(slot1_s, recv1, x1, n_one)
    rows = 128

    def first_layer(b, _):
        f = pl.multiple_of(b * rows, rows)
        own = jnp.concatenate(
            [x1[pl.ds(2 * f, rows, stride=2), :], x1[pl.ds(2 * f + 1, rows, stride=2), :]], axis=1
        ).astype(BF16)
        total = jnp.dot(own, wf[:width, :], preferred_element_type=F32)
        total = total + jnp.dot(
            min1[pl.ds(f, rows), :], wf[width:, :], preferred_element_type=F32
        )
        out = jnp.maximum(total, 0.0).astype(BF16).astype(F32)
        h1l[pl.ds(f, rows), :] = out[:, :LANES]
        h1r[pl.ds(f, rows), :] = out[:, LANES:]
        return 0

    lax.fori_loop(0, n_one // rows, first_layer, 0)

    def four_means(load):
        def some(b, _):
            s = pl.multiple_of(b * tile, tile)
            rels = [relc1[pl.ds(FAN1 * s + j, tile, stride=FAN1), :] for j in range(FAN1)]
            for r in range(R):
                hits = [rel == r for rel in rels]
                tally = sum(jnp.where(hit, 1.0, 0.0) for hit in hits)
                share = jnp.where(
                    tally == 4.0, 0.25, jnp.where(tally == 3.0, 1.0 / 3.0, jnp.where(tally == 2.0, 0.5, 1.0))
                )
                for half in range(2):
                    total = sum(
                        jnp.where(hits[j], load(s, j, half), 0.0) for j in range(FAN1)
                    )
                    at = r * width + half * LANES
                    min0[pl.ds(s, tile), at : at + LANES] = (total * share).astype(BF16)
            return 0

        lax.fori_loop(0, n_seed // tile, some, 0)

    four_means(lambda s, j, half: x1[pl.ds(8 * s + 2 * j + half, tile, stride=8), :])
    seed_part = jnp.dot(min0[...], wf[width:, :], preferred_element_type=F32)
    four_means(
        lambda s, j, half: (h1l, h1r)[half][pl.ds(FAN1 * s + j, tile, stride=FAN1), :]
    )
    second_part = jnp.dot(min0[...], ws[width:, :], preferred_element_type=F32)

    arrived(0, recv0, cap0)
    unpack(slot0_s, recv0, x0, n_seed)
    own = jnp.concatenate(
        [x0[pl.ds(0, n_seed, stride=2), :], x0[pl.ds(1, n_seed, stride=2), :]], axis=1
    ).astype(BF16)
    h1s = jnp.maximum(
        jnp.dot(own, wf[:width, :], preferred_element_type=F32) + seed_part, 0.0
    ).astype(BF16)
    second = jnp.dot(h1s, ws[:width, :], preferred_element_type=F32) + second_part

    edges = mask_ref.shape[1]
    sources = second[:edges]
    products = sources * second[edges : 2 * edges]
    positive = lax.dot_general(
        jnp.ones((8, width), F32), products, NT,
        precision=lax.Precision.HIGHEST, preferred_element_type=F32,
    )[:1]
    negative = lax.dot_general(
        second[2 * edges :], sources, NT,
        precision=lax.Precision.HIGHEST, preferred_element_type=F32,
    )
    top = jnp.maximum(jnp.max(negative, axis=0, keepdims=True), positive)
    spread = jnp.sum(jnp.exp(negative - top), axis=0, keepdims=True) + jnp.exp(positive - top)
    edge_loss = top + jnp.log(spread) - positive
    loss_ref[...] = edge_loss
    weights = mask_ref[...].astype(F32)
    both = jnp.concatenate([weights * edge_loss, weights], axis=0)
    part_out[...] = both
    part_in[me] = both

    def tell(k, _):
        pltpu.make_async_remote_copy(
            src_ref=part_out, dst_ref=part_in.at[me], send_sem=psend, recv_sem=precv,
            device_id=target(k), device_id_type=LOGICAL,
        ).start()
        return 0

    sent = req_out.at[rest]
    pltpu.make_async_copy(sent, sent, qsend).wait()
    for out, _, cap, _, h in hops:
        sent = out.at[pl.ds(0, (n - 1) * cap)]
        pltpu.make_async_copy(sent, sent, ssem.at[h]).wait()
    lax.fori_loop(1, n, tell, 0)
    told = part_in.at[rest]
    pltpu.make_async_copy(told, told, precv).wait()
    sums = jnp.sum(jnp.sum(part_in[...], axis=0), axis=1, keepdims=True)
    mean_ref[...] = jnp.broadcast_to(
        sums[:1] / jnp.maximum(sums[1:], 1.0), mean_ref.shape
    )
    pltpu.make_async_copy(told, told, psend).wait()


def solution(mesh):
    n = mesh.shape["dom"]

    def shards(
        features, w_first, w_second, seed_owner, seed_row, hop1_owner, hop1_row, hop1_rel,
        hop2_owner, hop2_row, hop2_rel, edge_mask,
    ):
        nodes, width = features.shape
        n_seed, n_one, n_two = seed_row.shape[0], hop1_row.shape[0], hop2_row.shape[0]
        edges = edge_mask.shape[0]
        caps = tuple(-(-2 * m // n) for m in (n_seed, n_one, n_two))
        cap0, cap1, cap2 = caps
        padded = -(-n_seed // LANES) * LANES
        vmem, hbm = pl.BlockSpec(memory_space=pltpu.VMEM), pl.BlockSpec(memory_space=pl.ANY)
        dma = pltpu.SemaphoreType.DMA

        def rows_of(cap):
            return pltpu.VMEM((n * cap, 2, LANES), BF16)

        def line(m):
            return pltpu.VMEM((1, m), jnp.int32)

        scratch = [
            line(n_seed), line(n_seed), line(n_one), line(n_one), line(n_one),
            line(n_two), line(n_two), line(n_two), line(edges),
            pltpu.VMEM((nodes, width), BF16),
            pltpu.VMEM((2 * nodes + 8, LANES), F32),
            pltpu.VMEM(w_first.shape, BF16),
            pltpu.VMEM(w_second.shape, BF16),
            pltpu.VMEM((1, padded), jnp.int32),
            pltpu.VMEM((1, padded), jnp.int32),
            pltpu.VMEM((1, padded), jnp.int32),
            pltpu.VMEM((1, n_one), jnp.int32),
            pltpu.VMEM((1, n_two), jnp.int32),
            pltpu.VMEM((n, 1, LANES), jnp.int32),
            pltpu.VMEM((n, 1, LANES), jnp.int32),
            rows_of(cap0), rows_of(cap1), rows_of(cap2),
            rows_of(cap0), rows_of(cap1), rows_of(cap2),
            pltpu.VMEM((2 * n_seed, LANES), F32),
            pltpu.VMEM((2 * n_one, LANES), F32),
            pltpu.VMEM((2 * n_two, LANES), F32),
            pltpu.VMEM((n_one, R * width), BF16),
            pltpu.VMEM((n_seed, R * width), BF16),
            pltpu.VMEM((n_one, LANES), F32),
            pltpu.VMEM((n_one, LANES), F32),
            pltpu.VMEM((n_one, LANES), F32),
            pltpu.VMEM((n_two, LANES), F32),
            pltpu.VMEM((2, edges), F32),
            pltpu.VMEM((n, 2, edges), F32),
            pltpu.SMEM((n, 1, LANES), jnp.int32),
            pltpu.SMEM((1, padded), jnp.int32),
            pltpu.SMEM((1, n_one), jnp.int32),
            pltpu.SMEM((1, n_two), jnp.int32),
            dma((9,)), dma((4,)), dma((2,)), dma, dma, dma((3,)), dma((3,)), dma((4,)), dma, dma,
        ]
        edge_loss, mean = pl.pallas_call(
            functools.partial(kernel, n, (n_seed, n_one, n_two), caps),
            out_shape=(
                jax.ShapeDtypeStruct((1, edges), F32),
                jax.ShapeDtypeStruct((1, LANES), F32),
            ),
            in_specs=[hbm] * 12,
            out_specs=(vmem, vmem),
            scratch_shapes=scratch,
            compiler_params=pltpu.CompilerParams(
                collective_id=0, has_side_effects=True, vmem_limit_bytes=62 * 2**20
            ),
            name="fetch_and_score",
        )(
            features, w_first, w_second,
            seed_owner.reshape(1, n_seed), seed_row,
            hop1_owner.reshape(1, n_one), hop1_row, hop1_rel,
            hop2_owner.reshape(1, n_two), hop2_row, hop2_rel, edge_mask,
        )
        return edge_loss.reshape(edges), mean[0, 0]

    dom = P("dom")
    tall = P("dom", None)
    return jax.shard_map(
        shards,
        mesh=mesh,
        in_specs=(tall, P(), P(), tall, dom, tall, dom, dom, tall, dom, dom, dom),
        out_specs=(dom, P()),
        check_vma=False,
    )
```

time: 209 us -> 89.8 us (0.43)
  Pallas kernels: 0 us -> 86.1 us
  local copies, waits for them, and re-layouts: 70.9 us -> 1.11 us
  blocking collectives: 52.1 us -> 0 us
  waiting for transfers between devices: 45.6 us -> 0 us
  matrix products: 17 us -> 0 us
  other arithmetic: 13.5 us -> 0 us
  starting transfers between devices: 5.45 us -> 0 us
    pallas_call x0 -> x1, Pallas kernels: none -> 86.1 us  [shards(): pl.pallas_call(functools.partial(kernel, n, (n_seed, n_one, n_two), caps)...]
    all_to_all x1 -> x0, waiting for transfers between devices: 45.6 us -> none  [shards(): lax.all_to_all(located, DOM, split_axis=0, concat_axis=0, tiled=True)]
    gather x4 -> x0, local copies, waits for them, and re-layouts: 36.4 us -> none  [the longest x1 22.7 us: shards(): located = features[arrived.reshape(-1)].reshape(devices, total_cap, width)]
    psum x4 -> x0, blocking collectives: 31.1 us -> none  [by_axis(): return functools.reduce(lax.psum, axes, value)]
    all_to_all x1 -> x0, blocking collectives: 20.9 us -> none  [shards(): lax.all_to_all(requests, DOM, split_axis=0, concat_axis=0, tiled=True)]
    dot_general x10 -> x0, matrix products: 17 us -> none  [the longest x3 9.86 us: bucket_rows(): lax.dot_general(slot_hot, halves, (((0,), (0,)), ((), ())), preferred_ele...]
    reshape x8 -> x0, local copies, waits for them, and re-layouts: 13.5 us -> none  [the longest x2 6.38 us: shards(): located = features[arrived.reshape(-1)].reshape(devices, total_cap, width)]
    slice x3 -> x0, local copies, waits for them, and re-layouts: 8.58 us -> none  [the longest x1 5 us: shards(): returned[:, cap_seed + cap_first:].reshape(devices * cap_second, width)]
  transfers between devices with their start and end apart: 1 -> 0, of which waited for: 1 -> 0; matrix products, arithmetic and copies ran while one was open for 3% -> 0% of each run, Pallas kernels for 0% -> 0%
where the time goes in v1:
time: 89.8 us; the launch traced here: 89.6 us
  Pallas kernels  86.1 us (96%)
  between operations  2.41 us (3%)
  local copies, waits for them, and re-layouts  1.11 us (1%)
    pallas_call x1, Pallas kernels, shards(): pl.pallas_call(functools.partial(kernel, n, (n_seed, n_one, n_two), caps)...  86.1 us

profile of v1, /device:TPU:1, one launch (start us, length us, event | category | flops | bytes accessed | tf_op | source)
XLA Modules:
  0.0 89.6 jit_solution(6148738719203031151)
XLA Ops:
  0.6 86.1 %fetch_and_score.1 = (f32[1,128]{1,0:T(1,128)}, f32[1,128]{1,0:T(1,128)}) custom-call(bf16[16384,256]{1,0:T(8,128)(2,1)} %feat_hbm.1, bf16[1280,256]{1,0:T(8,128)(2,1)} %wf_hbm.1, bf16[1280,256]{1,0:T(8,128)(2,1)} %ws_hbm.1, s32[1,288]{1,0:T(1,128)} %bitcast.8, s32[288]{0:T(512)} %row0_hbm.1, s32[1,1152]{1,0:T(1,128)} %bitcast.7, s32[1152]{0:T(1024)} %row1_hbm.1, ...), custom_call_target="tpu_custom_call" | custom-call | tf_op jit(solution)/shard_map/fetch_and_score/pallas_call | solution.py:404
  86.8 1.1 %copy.16 = f32[128]{0:T(128)} copy(f32[128]{0:T(128)} %bitcast.10) | data formatting | bytes 1024

commit v2 on v1

--- a/solution.py
+++ b/solution.py
@@ -1,4 +1,5 @@
 import functools
+import itertools
 
 import jax
 import jax.numpy as jnp
@@ -11,6 +12,7 @@
 FAN1 = 4
 FAN2 = 2
 LANES = 128
+SIDE = 4
 STEP = 45
 LOGICAL = pl.DeviceIdType.LOGICAL
 F32 = jnp.float32
@@ -41,6 +43,19 @@
     def target(k):
         return lax.rem(me + lax.rem(k * STEP, n), n)
 
+    side = SIDE
+    spots = []
+    scale = n
+    for length in (side, side, side, 2):
+        scale //= length
+        at = lax.rem(lax.div(me, scale), length)
+        spots.append([lax.rem(at + d, length) * scale for d in range(length)])
+    offsets = sorted(
+        itertools.product(range(side), range(side), range(side), range(2)),
+        key=lambda o: (-sum(min(d, side - d) for d in o[:3]), o),
+    )
+    peers = [sum(spot[d] for spot, d in zip(spots, o)) for o in offsets if any(o)]
+
     here_refs = (own2, row2, own1, row1, own0, row0, rel2, rel1, mask_ref)
     there_refs = (
         own2_hbm, row2_hbm, own1_hbm, row1_hbm, own0_hbm, row0_hbm, rel2_hbm, rel1_hbm, mask_hbm
@@ -54,11 +69,8 @@
 
     barrier = pltpu.get_barrier_semaphore()
 
-    def greet(k, _):
-        pl.semaphore_signal(barrier, 1, device_id=target(k), device_id_type=LOGICAL)
-        return 0
-
-    lax.fori_loop(1, n, greet, 0)
+    for t in peers:
+        pl.semaphore_signal(barrier, 1, device_id=t, device_id_type=LOGICAL)
     chunks = fsem.shape[0]
     part = nodes // chunks
     feat_copies = [
@@ -108,7 +120,7 @@
             return before + counts[:, LANES:], table
 
         zero = jnp.zeros((n, LANES), F32)
-        return lax.fori_loop(0, blocks, block, (zero, table))[1]
+        return lax.fori_loop(0, blocks, block, (zero, table), unroll=3)[1]
 
     for copy in index_copies[:6]:
         copy.wait()
@@ -139,15 +151,11 @@
 
     pl.semaphore_wait(barrier, n - 1)
 
-    def ask(k, _):
-        t = target(k)
+    for t in peers:
         pltpu.make_async_remote_copy(
             src_ref=req_out.at[t], dst_ref=req_in.at[me], send_sem=qsend, recv_sem=qrecv,
             device_id=t, device_id_type=LOGICAL,
         ).start()
-        return 0
-
-    lax.fori_loop(1, n, ask, 0)
     req_in[me] = req_out[me]
 
     for i in range(1, chunks):
@@ -320,29 +328,29 @@
     edge_loss = top + jnp.log(spread) - positive
     loss_ref[...] = edge_loss
     weights = mask_ref[...].astype(F32)
-    both = jnp.concatenate([weights * edge_loss, weights], axis=0)
+    left = lax.broadcasted_iota(jnp.int32, weights.shape, 1) < LANES // 2
+    masked = weights * edge_loss
+    both = jnp.where(
+        left, masked + pltpu.roll(masked, LANES // 2, 1), weights + pltpu.roll(weights, LANES // 2, 1)
+    )
     part_out[...] = both
     part_in[me] = both
-
-    def tell(k, _):
-        pltpu.make_async_remote_copy(
-            src_ref=part_out, dst_ref=part_in.at[me], send_sem=psend, recv_sem=precv,
-            device_id=target(k), device_id_type=LOGICAL,
-        ).start()
-        return 0
-
     sent = req_out.at[rest]
     pltpu.make_async_copy(sent, sent, qsend).wait()
     for out, _, cap, _, h in hops:
         sent = out.at[pl.ds(0, (n - 1) * cap)]
         pltpu.make_async_copy(sent, sent, ssem.at[h]).wait()
-    lax.fori_loop(1, n, tell, 0)
+    for t in peers:
+        pltpu.make_async_remote_copy(
+            src_ref=part_out, dst_ref=part_in.at[me], send_sem=psend, recv_sem=precv,
+            device_id=t, device_id_type=LOGICAL,
+        ).start()
     told = part_in.at[rest]
     pltpu.make_async_copy(told, told, precv).wait()
-    sums = jnp.sum(jnp.sum(part_in[...], axis=0), axis=1, keepdims=True)
-    mean_ref[...] = jnp.broadcast_to(
-        sums[:1] / jnp.maximum(sums[1:], 1.0), mean_ref.shape
-    )
+    total = jnp.sum(part_in[...], axis=0)
+    loss_sum = jnp.sum(jnp.where(left, total, 0.0), axis=1, keepdims=True)
+    tally = jnp.sum(jnp.where(left, 0.0, total), axis=1, keepdims=True)
+    mean_ref[...] = jnp.broadcast_to(loss_sum / jnp.maximum(tally, 1.0), mean_ref.shape)
     pltpu.make_async_copy(told, told, psend).wait()
 
 
@@ -393,8 +401,8 @@
             pltpu.VMEM((n_one, LANES), F32),
             pltpu.VMEM((n_one, LANES), F32),
             pltpu.VMEM((n_two, LANES), F32),
-            pltpu.VMEM((2, edges), F32),
-            pltpu.VMEM((n, 2, edges), F32),
+            pltpu.VMEM((1, edges), F32),
+            pltpu.VMEM((n, 1, edges), F32),
             pltpu.SMEM((n, 1, LANES), jnp.int32),
             pltpu.SMEM((1, padded), jnp.int32),
             pltpu.SMEM((1, n_one), jnp.int32),

time: 89.8 us -> 79.3 us (0.88)
  Pallas kernels: 86.1 us -> 75.7 us
    pallas_call x1, Pallas kernels: 86.1 us -> 75.7 us  [shards(): pl.pallas_call(functools.partial(kernel, n, (n_seed, n_one, n_two), caps)...]
where the time goes in v2:
time: 79.3 us; the launch traced here: 79.2 us
  Pallas kernels  75.7 us (95%)
  between operations  2.41 us (3%)
  local copies, waits for them, and re-layouts  1.11 us (1%)
    pallas_call x1, Pallas kernels, shards(): pl.pallas_call(functools.partial(kernel, n, (n_seed, n_one, n_two), caps)...  75.7 us

profile of v2, /device:TPU:1, one launch (start us, length us, event | category | flops | bytes accessed | tf_op | source)
XLA Modules:
  0.0 79.2 jit_solution(14985933485794459494)
XLA Ops:
  0.6 75.7 %fetch_and_score.1 = (f32[1,128]{1,0:T(1,128)}, f32[1,128]{1,0:T(1,128)}) custom-call(bf16[16384,256]{1,0:T(8,128)(2,1)} %feat_hbm.1, bf16[1280,256]{1,0:T(8,128)(2,1)} %wf_hbm.1, bf16[1280,256]{1,0:T(8,128)(2,1)} %ws_hbm.1, s32[1,288]{1,0:T(1,128)} %bitcast.8, s32[288]{0:T(512)} %row0_hbm.1, s32[1,1152]{1,0:T(1,128)} %bitcast.7, s32[1152]{0:T(1024)} %row1_hbm.1, ...), custom_call_target="tpu_custom_call" | custom-call | tf_op jit(solution)/shard_map/fetch_and_score/pallas_call | solution.py:412
  76.3 1.1 %copy.16 = f32[128]{0:T(128)} copy(f32[128]{0:T(128)} %bitcast.10) | data formatting | bytes 1024

commit v3 on v2

--- a/solution.py
+++ b/solution.py
@@ -13,7 +13,7 @@
 FAN2 = 2
 LANES = 128
 SIDE = 4
-STEP = 45
+NEAR = 2
 LOGICAL = pl.DeviceIdType.LOGICAL
 F32 = jnp.float32
 BF16 = jnp.bfloat16
@@ -27,9 +27,9 @@
     loss_ref, mean_ref,
     own0, row0, own1, row1, rel1, own2, row2, rel2, mask_ref,
     fbf, fsp, wf, ws, pad_own, pad_row, slots0, slots1, slots2, req_out, req_in,
-    send0, send1, send2, recv0, recv1, recv2, x0, x1, x2, min1, min0, h1l, h1r, relc1, relc2,
+    send0, send1, send2, recv0, recv1, recv2, x0, x1, x2, min1, min0, pre1, h1l, h1r, relc1, relc2,
     part_out, part_in,
-    req_s, slot0_s, slot1_s, slot2_s,
+    req_s, asker_s, slot0_s, slot1_s, slot2_s,
     isem, fsem, wsem, qsend, qrecv, ssem, rsem, tsem, psend, precv,
 ):
     n_seed, n_one, n_two = count
@@ -40,21 +40,27 @@
     nodes = fbf.shape[0]
     gap = fsp.shape[0] - nodes
 
-    def target(k):
-        return lax.rem(me + lax.rem(k * STEP, n), n)
-
-    side = SIDE
+    lengths = (SIDE, SIDE, SIDE, 2)
     spots = []
     scale = n
-    for length in (side, side, side, 2):
+    for length in lengths:
         scale //= length
         at = lax.rem(lax.div(me, scale), length)
         spots.append([lax.rem(at + d, length) * scale for d in range(length)])
+
+    def hops_of(o):
+        return sum(min(d, SIDE - d) for d in o[:3])
+
     offsets = sorted(
-        itertools.product(range(side), range(side), range(side), range(2)),
-        key=lambda o: (-sum(min(d, side - d) for d in o[:3]), o),
-    )
-    peers = [sum(spot[d] for spot, d in zip(spots, o)) for o in offsets if any(o)]
+        itertools.product(*(range(length) for length in lengths)), key=lambda o: (hops_of(o) > NEAR, any(o), (((o[0] * 4 + o[1]) * 4 + o[2]) * 2 + o[3]) * 109 % 128)
+    )
+    close = sum(hops_of(o) <= NEAR for o in offsets)
+
+    def at_offset(o):
+        return sum(spot[d] for spot, d in zip(spots, o))
+
+    peers = [at_offset(o) for o in offsets]
+    askers = [at_offset([-d % m for d, m in zip(o, lengths)]) for o in offsets]
 
     here_refs = (own2, row2, own1, row1, own0, row0, rel2, rel1, mask_ref)
     there_refs = (
@@ -69,8 +75,10 @@
 
     barrier = pltpu.get_barrier_semaphore()
 
-    for t in peers:
+    for t in peers[:0:-1]:
         pl.semaphore_signal(barrier, 1, device_id=t, device_id_type=LOGICAL)
+    for k in range(n):
+        asker_s[0, k] = askers[k]
     chunks = fsem.shape[0]
     part = nodes // chunks
     feat_copies = [
@@ -120,7 +128,7 @@
             return before + counts[:, LANES:], table
 
         zero = jnp.zeros((n, LANES), F32)
-        return lax.fori_loop(0, blocks, block, (zero, table), unroll=3)[1]
+        return lax.fori_loop(0, blocks, block, (zero, table), unroll=9 if blocks % 9 == 0 else 3)[1]
 
     for copy in index_copies[:6]:
         copy.wait()
@@ -151,54 +159,69 @@
 
     pl.semaphore_wait(barrier, n - 1)
 
-    for t in peers:
+    for k in range(n - 1, 0, -1):
+        t = peers[k]
         pltpu.make_async_remote_copy(
-            src_ref=req_out.at[t], dst_ref=req_in.at[me], send_sem=qsend, recv_sem=qrecv,
-            device_id=t, device_id_type=LOGICAL,
+            src_ref=req_out.at[t], dst_ref=req_in.at[k], send_sem=qsend,
+            recv_sem=qrecv.at[0 if k < close else 1], device_id=t, device_id_type=LOGICAL,
         ).start()
-    req_in[me] = req_out[me]
+    req_in[0] = req_out[me]
 
     for i in range(1, chunks):
         feat_copies[i].wait()
         lax.fori_loop(i * per_chunk, (i + 1) * per_chunk, widen, 0)
 
+    def asked(first, last, i):
+        got = req_in.at[pl.ds(max(first, 1), last - max(first, 1))]
+        pltpu.make_async_copy(got, got, qrecv.at[i]).wait()
+        group = pl.ds(first, last - first)
+        copy = pltpu.make_async_copy(req_in.at[group], req_s.at[group], tsem.at[i])
+        copy.start()
+        copy.wait()
+
     rest = pl.ds(0, n - 1)
-    pltpu.make_async_copy(req_in.at[rest], req_in.at[rest], qrecv).wait()
-    small = [
-        pltpu.make_async_copy(req_in, req_s, tsem.at[0]),
-        pltpu.make_async_copy(slots2, slot2_s, tsem.at[1]),
-        pltpu.make_async_copy(slots1, slot1_s, tsem.at[2]),
-        pltpu.make_async_copy(slots0, slot0_s, tsem.at[3]),
+    slot_copies = [
+        pltpu.make_async_copy(slots2, slot2_s, tsem.at[2]),
+        pltpu.make_async_copy(slots1, slot1_s, tsem.at[3]),
+        pltpu.make_async_copy(slots0, slot0_s, tsem.at[4]),
     ]
-    for copy in small:
-        copy.start()
-    small[0].wait()
+    asked(0, close, 0)
 
     hops = ((send2, recv2, cap2, bases[2], 2), (send1, recv1, cap1, bases[1], 1), (send0, recv0, cap0, bases[0], 0))
 
-    def gather(t, out, cap, base):
+    def gather(k, out, at, cap, base):
         for j in range(cap):
-            node = req_s[t, 0, base + j]
+            node = req_s[k, 0, base + j]
             pair = fsp[pl.ds(node, 2, stride=gap), :]
-            out[t * cap + j] = pair.astype(BF16)
-
-    def start_send(t, out, into, cap, h):
+            out[at * cap + j] = pair.astype(BF16)
+
+    def start_send(k, out, into, cap, h):
+        t = asker_s[0, k]
         pltpu.make_async_remote_copy(
-            src_ref=out.at[pl.ds(t * cap, cap)], dst_ref=into.at[pl.ds(me * cap, cap)],
+            src_ref=out.at[pl.ds(k * cap, cap)], dst_ref=into.at[pl.ds(me * cap, cap)],
             send_sem=ssem.at[h], recv_sem=rsem.at[h], device_id=t, device_id_type=LOGICAL,
         ).start()
 
-    for out, into, cap, base, h in hops:
-
-        def serve(k, _, out=out, into=into, cap=cap, base=base, h=h):
-            gather(target(k), out, cap, base)
-            start_send(target(k - 1), out, into, cap, h)
+    def serve(first, last, out, into, cap, base, h):
+        def one(k, _):
+            gather(k, out, k, cap, base)
+            start_send(k - 1, out, into, cap, h)
             return 0
 
-        gather(target(1), out, cap, base)
-        lax.fori_loop(2, n, serve, 0)
-        gather(me, into, cap, base)
-        start_send(target(n - 1), out, into, cap, h)
+        gather(first, out, first, cap, base)
+        lax.fori_loop(first + 1, last, one, 0)
+        start_send(last - 1, out, into, cap, h)
+
+    out, into, cap, base, h = hops[0]
+    serve(1, close, *hops[0])
+    asked(close, n, 1)
+    for copy in slot_copies:
+        copy.start()
+    serve(close, n, *hops[0])
+    gather(0, into, me, cap, base)
+    for out, into, cap, base, h in hops[1:]:
+        serve(1, n, out, into, cap, base, h)
+        gather(0, into, me, cap, base)
 
     for copy in index_copies[6:]:
         copy.wait()
@@ -214,7 +237,7 @@
 
     relation_columns(rel2, relc2, n_two // LANES)
     relation_columns(rel1, relc1, n_one // LANES)
-    for copy in small[1:]:
+    for copy in slot_copies:
         copy.wait()
     for copy in w_copies:
         copy.wait()
@@ -255,9 +278,18 @@
 
     lax.fori_loop(0, n_one // tile, two_means, 0)
 
+    def mean_part(b, _):
+        f = pl.multiple_of(b * rows, rows)
+        pre1[pl.ds(f, rows), :] = jnp.dot(
+            min1[pl.ds(f, rows), :], wf[width:, :], preferred_element_type=F32
+        )
+        return 0
+
+    rows = 128
+    lax.fori_loop(0, n_one // rows, mean_part, 0, unroll=3)
+
     arrived(1, recv1, cap1)
     unpack(slot1_s, recv1, x1, n_one)
-    rows = 128
 
     def first_layer(b, _):
         f = pl.multiple_of(b * rows, rows)
@@ -265,15 +297,13 @@
             [x1[pl.ds(2 * f, rows, stride=2), :], x1[pl.ds(2 * f + 1, rows, stride=2), :]], axis=1
         ).astype(BF16)
         total = jnp.dot(own, wf[:width, :], preferred_element_type=F32)
-        total = total + jnp.dot(
-            min1[pl.ds(f, rows), :], wf[width:, :], preferred_element_type=F32
-        )
+        total = total + pre1[pl.ds(f, rows), :]
         out = jnp.maximum(total, 0.0).astype(BF16).astype(F32)
         h1l[pl.ds(f, rows), :] = out[:, :LANES]
         h1r[pl.ds(f, rows), :] = out[:, LANES:]
         return 0
 
-    lax.fori_loop(0, n_one // rows, first_layer, 0)
+    lax.fori_loop(0, n_one // rows, first_layer, 0, unroll=3)
 
     def four_means(load):
         def some(b, _):
@@ -293,7 +323,7 @@
                     min0[pl.ds(s, tile), at : at + LANES] = (total * share).astype(BF16)
             return 0
 
-        lax.fori_loop(0, n_seed // tile, some, 0)
+        lax.fori_loop(0, n_seed // tile, some, 0, unroll=3)
 
     four_means(lambda s, j, half: x1[pl.ds(8 * s + 2 * j + half, tile, stride=8), :])
     seed_part = jnp.dot(min0[...], wf[width:, :], preferred_element_type=F32)
@@ -335,12 +365,7 @@
     )
     part_out[...] = both
     part_in[me] = both
-    sent = req_out.at[rest]
-    pltpu.make_async_copy(sent, sent, qsend).wait()
-    for out, _, cap, _, h in hops:
-        sent = out.at[pl.ds(0, (n - 1) * cap)]
-        pltpu.make_async_copy(sent, sent, ssem.at[h]).wait()
-    for t in peers:
+    for t in peers[:0:-1]:
         pltpu.make_async_remote_copy(
             src_ref=part_out, dst_ref=part_in.at[me], send_sem=psend, recv_sem=precv,
             device_id=t, device_id_type=LOGICAL,
@@ -352,6 +377,11 @@
     tally = jnp.sum(jnp.where(left, 0.0, total), axis=1, keepdims=True)
     mean_ref[...] = jnp.broadcast_to(loss_sum / jnp.maximum(tally, 1.0), mean_ref.shape)
     pltpu.make_async_copy(told, told, psend).wait()
+    sent = req_out.at[rest]
+    pltpu.make_async_copy(sent, sent, qsend).wait()
+    for out, _, cap, _, h in hops:
+        sent = out.at[pl.ds(0, (n - 1) * cap)]
+        pltpu.make_async_copy(sent, sent, ssem.at[h]).wait()
 
 
 def solution(mesh):
@@ -397,6 +427,7 @@
             pltpu.VMEM((2 * n_two, LANES), F32),
             pltpu.VMEM((n_one, R * width), BF16),
             pltpu.VMEM((n_seed, R * width), BF16),
+            pltpu.VMEM((n_one, width), F32),
             pltpu.VMEM((n_one, LANES), F32),
             pltpu.VMEM((n_one, LANES), F32),
             pltpu.VMEM((n_one, LANES), F32),
@@ -404,10 +435,11 @@
             pltpu.VMEM((1, edges), F32),
             pltpu.VMEM((n, 1, edges), F32),
             pltpu.SMEM((n, 1, LANES), jnp.int32),
+            pltpu.SMEM((1, n), jnp.int32),
             pltpu.SMEM((1, padded), jnp.int32),
             pltpu.SMEM((1, n_one), jnp.int32),
             pltpu.SMEM((1, n_two), jnp.int32),
-            dma((9,)), dma((4,)), dma((2,)), dma, dma, dma((3,)), dma((3,)), dma((4,)), dma, dma,
+            dma((9,)), dma((4,)), dma((2,)), dma, dma((2,)), dma((3,)), dma((3,)), dma((5,)), dma, dma,
         ]
         edge_loss, mean = pl.pallas_call(
             functools.partial(kernel, n, (n_seed, n_one, n_two), caps),

time: 79.3 us -> 75.5 us (0.952)
  Pallas kernels: 75.7 us -> 71.8 us
    pallas_call x1, Pallas kernels: 75.7 us -> 71.8 us  [shards(): pl.pallas_call(functools.partial(kernel, n, (n_seed, n_one, n_two), caps)...]
where the time goes in v3:
time: 75.5 us; the launch traced here: 75.3 us
  Pallas kernels  71.8 us (95%)
  between operations  2.41 us (3%)
  local copies, waits for them, and re-layouts  1.11 us (1%)
    pallas_call x1, Pallas kernels, shards(): pl.pallas_call(functools.partial(kernel, n, (n_seed, n_one, n_two), caps)...  71.8 us

profile of v3, /device:TPU:1, one launch (start us, length us, event | category | flops | bytes accessed | tf_op | source)
XLA Modules:
  0.0 75.3 jit_solution(11629834444685517969)
XLA Ops:
  0.6 71.8 %fetch_and_score.1 = (f32[1,128]{1,0:T(1,128)}, f32[1,128]{1,0:T(1,128)}) custom-call(bf16[16384,256]{1,0:T(8,128)(2,1)} %feat_hbm.1, bf16[1280,256]{1,0:T(8,128)(2,1)} %wf_hbm.1, bf16[1280,256]{1,0:T(8,128)(2,1)} %ws_hbm.1, s32[1,288]{1,0:T(1,128)} %bitcast.8, s32[288]{0:T(512)} %row0_hbm.1, s32[1,1152]{1,0:T(1,128)} %bitcast.7, s32[1152]{0:T(1024)} %row1_hbm.1, ...), custom_call_target="tpu_custom_call" | custom-call | tf_op jit(solution)/shard_map/fetch_and_score/pallas_call | solution.py:444
  72.5 1.1 %copy.16 = f32[128]{0:T(128)} copy(f32[128]{0:T(128)} %bitcast.10) | data formatting | bytes 1024

commit v4 on v3

--- a/solution.py
+++ b/solution.py
@@ -27,7 +27,7 @@
     loss_ref, mean_ref,
     own0, row0, own1, row1, rel1, own2, row2, rel2, mask_ref,
     fbf, fsp, wf, ws, pad_own, pad_row, slots0, slots1, slots2, req_out, req_in,
-    send0, send1, send2, recv0, recv1, recv2, x0, x1, x2, min1, min0, pre1, h1l, h1r, relc1, relc2,
+    send0, send1, send2, recv0, recv1, recv2, x0, x1, x2, min1, min0x, min0h, pre1, pick1, share1, relc2,
     part_out, part_in,
     req_s, asker_s, slot0_s, slot1_s, slot2_s,
     isem, fsem, wsem, qsend, qrecv, ssem, rsem, tsem, psend, precv,
@@ -159,7 +159,7 @@
 
     pl.semaphore_wait(barrier, n - 1)
 
-    for k in range(n - 1, 0, -1):
+    for k in range(1, n):
         t = peers[k]
         pltpu.make_async_remote_copy(
             src_ref=req_out.at[t], dst_ref=req_in.at[k], send_sem=qsend,
@@ -211,6 +211,17 @@
         gather(first, out, first, cap, base)
         lax.fori_loop(first + 1, last, one, 0)
         start_send(last - 1, out, into, cap, h)
+
+    def serve_back(first, last, out, into, cap, base, h):
+        def one(i, _):
+            k = last - 1 - i
+            gather(k, out, k, cap, base)
+            start_send(k + 1, out, into, cap, h)
+            return 0
+
+        gather(last - 1, out, last - 1, cap, base)
+        lax.fori_loop(1, last - first, one, 0)
+        start_send(first, out, into, cap, h)
 
     out, into, cap, base, h = hops[0]
     serve(1, close, *hops[0])
@@ -236,7 +247,25 @@
         lax.fori_loop(0, blocks, block, 0)
 
     relation_columns(rel2, relc2, n_two // LANES)
-    relation_columns(rel1, relc1, n_one // LANES)
+
+    def seed_picks(b, _):
+        at = pl.multiple_of(b * LANES, LANES)
+        rel = rel1[:, pl.ds(at, LANES)]
+        shape = (LANES // FAN1, LANES)
+        first = lax.broadcasted_iota(jnp.int32, shape, 0) * FAN1
+        ahead = lax.broadcasted_iota(jnp.int32, shape, 1) - first
+        mine = (ahead >= 0) & (ahead < FAN1)
+        pick = jnp.concatenate(
+            [jnp.where(mine & (rel == r), 1.0, 0.0) for r in range(R)], axis=0
+        ).astype(BF16)
+        pick1[pl.ds(at, LANES), :] = pick
+        tally = jnp.dot(pick, jnp.ones((LANES, LANES), BF16), preferred_element_type=F32)
+        share1[pl.ds(at, LANES), :] = jnp.where(
+            tally == 4.0, 0.25, jnp.where(tally == 3.0, 1.0 / 3.0, jnp.where(tally == 2.0, 0.5, 1.0))
+        )
+        return 0
+
+    lax.fori_loop(0, n_one // LANES, seed_picks, 0)
     for copy in slot_copies:
         copy.wait()
     for copy in w_copies:
@@ -298,39 +327,22 @@
         ).astype(BF16)
         total = jnp.dot(own, wf[:width, :], preferred_element_type=F32)
         total = total + pre1[pl.ds(f, rows), :]
-        out = jnp.maximum(total, 0.0).astype(BF16).astype(F32)
-        h1l[pl.ds(f, rows), :] = out[:, :LANES]
-        h1r[pl.ds(f, rows), :] = out[:, LANES:]
+        out = jnp.maximum(total, 0.0).astype(BF16)
+        pick = pick1[pl.ds(f, rows), :]
+        share = share1[pl.ds(f, rows), :]
+        s = pl.multiple_of(b * tile, tile)
+        for values, means in ((own, min0x), (out, min0h)):
+            sums = jnp.dot(pick, values, preferred_element_type=F32)
+            for r in range(R):
+                for at in range(0, width, LANES):
+                    mean = sums[r * tile : (r + 1) * tile, at : at + LANES] * share[r * tile : (r + 1) * tile]
+                    means[pl.ds(s, tile), r * width + at : r * width + at + LANES] = mean.astype(BF16)
         return 0
 
     lax.fori_loop(0, n_one // rows, first_layer, 0, unroll=3)
 
-    def four_means(load):
-        def some(b, _):
-            s = pl.multiple_of(b * tile, tile)
-            rels = [relc1[pl.ds(FAN1 * s + j, tile, stride=FAN1), :] for j in range(FAN1)]
-            for r in range(R):
-                hits = [rel == r for rel in rels]
-                tally = sum(jnp.where(hit, 1.0, 0.0) for hit in hits)
-                share = jnp.where(
-                    tally == 4.0, 0.25, jnp.where(tally == 3.0, 1.0 / 3.0, jnp.where(tally == 2.0, 0.5, 1.0))
-                )
-                for half in range(2):
-                    total = sum(
-                        jnp.where(hits[j], load(s, j, half), 0.0) for j in range(FAN1)
-                    )
-                    at = r * width + half * LANES
-                    min0[pl.ds(s, tile), at : at + LANES] = (total * share).astype(BF16)
-            return 0
-
-        lax.fori_loop(0, n_seed // tile, some, 0, unroll=3)
-
-    four_means(lambda s, j, half: x1[pl.ds(8 * s + 2 * j + half, tile, stride=8), :])
-    seed_part = jnp.dot(min0[...], wf[width:, :], preferred_element_type=F32)
-    four_means(
-        lambda s, j, half: (h1l, h1r)[half][pl.ds(FAN1 * s + j, tile, stride=FAN1), :]
-    )
-    second_part = jnp.dot(min0[...], ws[width:, :], preferred_element_type=F32)
+    seed_part = jnp.dot(min0x[...], wf[width:, :], preferred_element_type=F32)
+    second_part = jnp.dot(min0h[...], ws[width:, :], preferred_element_type=F32)
 
     arrived(0, recv0, cap0)
     unpack(slot0_s, recv0, x0, n_seed)
@@ -427,9 +439,9 @@
             pltpu.VMEM((2 * n_two, LANES), F32),
             pltpu.VMEM((n_one, R * width), BF16),
             pltpu.VMEM((n_seed, R * width), BF16),
+            pltpu.VMEM((n_seed, R * width), BF16),
             pltpu.VMEM((n_one, width), F32),
-            pltpu.VMEM((n_one, LANES), F32),
-            pltpu.VMEM((n_one, LANES), F32),
+            pltpu.VMEM((n_one, LANES), BF16),
             pltpu.VMEM((n_one, LANES), F32),
             pltpu.VMEM((n_two, LANES), F32),
             pltpu.VMEM((1, edges), F32),

time: 75.5 us -> 73.7 us (0.976)
  Pallas kernels: 71.8 us -> 70.1 us
    pallas_call x1, Pallas kernels: 71.8 us -> 70.1 us  [shards(): pl.pallas_call(functools.partial(kernel, n, (n_seed, n_one, n_two), caps)...]
where the time goes in v4:
time: 73.7 us; the launch traced here: 73.6 us
  Pallas kernels  70.1 us (95%)
  between operations  2.41 us (3%)
  local copies, waits for them, and re-layouts  1.11 us (2%)
    pallas_call x1, Pallas kernels, shards(): pl.pallas_call(functools.partial(kernel, n, (n_seed, n_one, n_two), caps)...  70.1 us

profile of v4, /device:TPU:1, one launch (start us, length us, event | category | flops | bytes accessed | tf_op | source)
XLA Modules:
  0.0 73.6 jit_solution(1082430385559257952)
XLA Ops:
  0.6 70.1 %fetch_and_score.1 = (f32[1,128]{1,0:T(1,128)}, f32[1,128]{1,0:T(1,128)}) custom-call(bf16[16384,256]{1,0:T(8,128)(2,1)} %feat_hbm.1, bf16[1280,256]{1,0:T(8,128)(2,1)} %wf_hbm.1, bf16[1280,256]{1,0:T(8,128)(2,1)} %ws_hbm.1, s32[1,288]{1,0:T(1,128)} %bitcast.8, s32[288]{0:T(512)} %row0_hbm.1, s32[1,1152]{1,0:T(1,128)} %bitcast.7, s32[1152]{0:T(1024)} %row1_hbm.1, ...), custom_call_target="tpu_custom_call" | custom-call | tf_op jit(solution)/shard_map/fetch_and_score/pallas_call | solution.py:456
  70.7 1.1 %copy.16 = f32[128]{0:T(128)} copy(f32[128]{0:T(128)} %bitcast.10) | data formatting | bytes 1024

commit v5 on v4

--- a/solution.py
+++ b/solution.py
@@ -24,7 +24,7 @@
     n, count, caps,
     feat_hbm, wf_hbm, ws_hbm,
     own0_hbm, row0_hbm, own1_hbm, row1_hbm, rel1_hbm, own2_hbm, row2_hbm, rel2_hbm, mask_hbm,
-    loss_ref, mean_ref,
+    result_ref,
     own0, row0, own1, row1, rel1, own2, row2, rel2, mask_ref,
     fbf, fsp, wf, ws, pad_own, pad_row, slots0, slots1, slots2, req_out, req_in,
     send0, send1, send2, recv0, recv1, recv2, x0, x1, x2, min1, min0x, min0h, pre1, pick1, share1, relc2,
@@ -41,26 +41,31 @@
     gap = fsp.shape[0] - nodes
 
     lengths = (SIDE, SIDE, SIDE, 2)
-    spots = []
-    scale = n
-    for length in lengths:
-        scale //= length
-        at = lax.rem(lax.div(me, scale), length)
-        spots.append([lax.rem(at + d, length) * scale for d in range(length)])
+    scales = [2 * SIDE * SIDE, 2 * SIDE, 2, 1]
+    ats = [lax.rem(lax.div(me, scale), length) for scale, length in zip(scales, lengths)]
+    core = ats[3]
+    toward, away = [], []
+    for sender in (core, 1 - core):
+        toward.append([])
+        away.append([])
+        for at, scale in zip(ats[:3], scales):
+            turn = [d + sender * (SIDE - 2 * d) for d in range(SIDE)]
+            toward[-1].append([lax.rem(at + t, SIDE) * scale for t in turn])
+            away[-1].append([lax.rem(at + 2 * SIDE - t, SIDE) * scale for t in turn])
 
     def hops_of(o):
         return sum(min(d, SIDE - d) for d in o[:3])
 
     offsets = sorted(
-        itertools.product(*(range(length) for length in lengths)), key=lambda o: (hops_of(o) > NEAR, any(o), (((o[0] * 4 + o[1]) * 4 + o[2]) * 2 + o[3]) * 109 % 128)
+        itertools.product(*(range(length) for length in lengths)), key=lambda o: (hops_of(o) > NEAR, any(o), (((o[0] * 4 + o[1]) * 4 + o[2]) * 2 + o[3]) * 45 % 128)
     )
     close = sum(hops_of(o) <= NEAR for o in offsets)
 
-    def at_offset(o):
-        return sum(spot[d] for spot, d in zip(spots, o))
-
-    peers = [at_offset(o) for o in offsets]
-    askers = [at_offset([-d % m for d, m in zip(o, lengths)]) for o in offsets]
+    def other(table, o):
+        return sum(spot[d] for spot, d in zip(table, o)) + (1 - core if o[3] else core)
+
+    peers = [other(toward[0], o) for o in offsets]
+    askers = [other(away[o[3]], o) for o in offsets]
 
     here_refs = (own2, row2, own1, row1, own0, row0, rel2, rel1, mask_ref)
     there_refs = (
@@ -73,12 +78,6 @@
     for copy in index_copies:
         copy.start()
 
-    barrier = pltpu.get_barrier_semaphore()
-
-    for t in peers[:0:-1]:
-        pl.semaphore_signal(barrier, 1, device_id=t, device_id_type=LOGICAL)
-    for k in range(n):
-        asker_s[0, k] = askers[k]
     chunks = fsem.shape[0]
     part = nodes // chunks
     feat_copies = [
@@ -89,6 +88,12 @@
     ]
     for copy in feat_copies:
         copy.start()
+    barrier = pltpu.get_barrier_semaphore()
+
+    for t in peers[:0:-1]:
+        pl.semaphore_signal(barrier, 1, device_id=t, device_id_type=LOGICAL)
+    for k in range(n):
+        asker_s[0, k] = askers[k]
     w_copies = [
         pltpu.make_async_copy(wf_hbm, wf, wsem.at[0]),
         pltpu.make_async_copy(ws_hbm, ws, wsem.at[1]),
@@ -368,7 +373,7 @@
     top = jnp.maximum(jnp.max(negative, axis=0, keepdims=True), positive)
     spread = jnp.sum(jnp.exp(negative - top), axis=0, keepdims=True) + jnp.exp(positive - top)
     edge_loss = top + jnp.log(spread) - positive
-    loss_ref[...] = edge_loss
+    result_ref[0:1, :] = edge_loss
     weights = mask_ref[...].astype(F32)
     left = lax.broadcasted_iota(jnp.int32, weights.shape, 1) < LANES // 2
     masked = weights * edge_loss
@@ -387,7 +392,7 @@
     total = jnp.sum(part_in[...], axis=0)
     loss_sum = jnp.sum(jnp.where(left, total, 0.0), axis=1, keepdims=True)
     tally = jnp.sum(jnp.where(left, 0.0, total), axis=1, keepdims=True)
-    mean_ref[...] = jnp.broadcast_to(loss_sum / jnp.maximum(tally, 1.0), mean_ref.shape)
+    result_ref[1:2, :] = jnp.broadcast_to(loss_sum / jnp.maximum(tally, 1.0), (1, LANES))
     pltpu.make_async_copy(told, told, psend).wait()
     sent = req_out.at[rest]
     pltpu.make_async_copy(sent, sent, qsend).wait()
@@ -453,14 +458,11 @@
             pltpu.SMEM((1, n_two), jnp.int32),
             dma((9,)), dma((4,)), dma((2,)), dma, dma((2,)), dma((3,)), dma((3,)), dma((5,)), dma, dma,
         ]
-        edge_loss, mean = pl.pallas_call(
+        result = pl.pallas_call(
             functools.partial(kernel, n, (n_seed, n_one, n_two), caps),
-            out_shape=(
-                jax.ShapeDtypeStruct((1, edges), F32),
-                jax.ShapeDtypeStruct((1, LANES), F32),
-            ),
+            out_shape=jax.ShapeDtypeStruct((2, LANES), F32),
             in_specs=[hbm] * 12,
-            out_specs=(vmem, vmem),
+            out_specs=vmem,
             scratch_shapes=scratch,
             compiler_params=pltpu.CompilerParams(
                 collective_id=0, has_side_effects=True, vmem_limit_bytes=62 * 2**20
@@ -472,7 +474,7 @@
             hop1_owner.reshape(1, n_one), hop1_row, hop1_rel,
             hop2_owner.reshape(1, n_two), hop2_row, hop2_rel, edge_mask,
         )
-        return edge_loss.reshape(edges), mean[0, 0]
+        return result[0], result[1, 0]
 
     dom = P("dom")
     tall = P("dom", None)

time: 73.7 us -> 73.1 us (level)
  between operations: 2.41 us -> 0.64 us
  local copies, waits for them, and re-layouts: 1.11 us -> 2.38 us
    slice x0 -> x1, local copies, waits for them, and re-layouts: none -> 1.19 us  [shards(): return (result[0], result[1, 0])]
    squeeze x0 -> x1, local copies, waits for them, and re-layouts: none -> 1.19 us  [shards(): return (result[0], result[1, 0])]
    unnamed x1 -> x0, local copies, waits for them, and re-layouts: 1.11 us -> none
where the time goes in v5:
time: 73.1 us; the launch traced here: 72.9 us
  Pallas kernels  69.9 us (96%)
  local copies, waits for them, and re-layouts  2.38 us (3%)
    pallas_call x1, Pallas kernels, shards(): pl.pallas_call(functools.partial(kernel, n, (n_seed, n_one, n_two), caps)...  69.9 us

profile of v5, /device:TPU:1, one launch (start us, length us, event | category | flops | bytes accessed | tf_op | source)
XLA Modules:
  0.0 72.9 jit_solution(6700524451713107691)
XLA Ops:
  0.6 69.9 %fetch_and_score.1 = f32[2,128]{1,0:T(2,128)} custom-call(bf16[16384,256]{1,0:T(8,128)(2,1)} %feat_hbm.1, bf16[1280,256]{1,0:T(8,128)(2,1)} %wf_hbm.1, bf16[1280,256]{1,0:T(8,128)(2,1)} %ws_hbm.1, s32[1,288]{1,0:T(1,128)} %bitcast.8, s32[288]{0:T(512)} %row0_hbm.1, s32[1,1152]{1,0:T(1,128)} %bitcast.7, s32[1152]{0:T(1024)} %row1_hbm.1, s32[1152]{0:T(1024)} %rel1_hbm.1, ...), custom_call_target="tpu_custom_call" | custom-call | tf_op jit(solution)/shard_map/fetch_and_score/pallas_call | solution.py:461
  70.6 1.2 %slice.7 = f32[1,1]{1,0:T(1,128)} slice(f32[2,128]{1,0:T(2,128)} %fetch_and_score.1), slice={[1:2], [0:1]} | slice | bytes 8 | tf_op jit(solution)/shard_map/slice | solution.py:477
  71.8 1.2 %slice_bitcast_fusion = f32[128]{0:T(128)} fusion(f32[2,128]{1,0:T(2,128)} %fetch_and_score.1), kind=kLoop, calls=%fused_computation | loop fusion | bytes 1024 | tf_op jit(solution)/shard_map/squeeze | solution.py:477
